TPU v7x, 32 devices: a whole 2x2x4 slice. The times are simulated.
32 devices in a mesh: groups: 2 (over y), kvb: 4 (over z), tp: 4 (over x, core).
Axes of the slice: x: 2, y: 2, z: 4, core: 2. Of those that a mesh axis runs over, the one named last changes fastest.
Arguments:
- residual: bfloat16 [32, 8192], P(('groups', 'kvb')), parts along dimension 0, may hold values from -3 to 3
- queries: bfloat16 [32, 8192], P(('groups', 'kvb'), 'tp'), parts along dimension 0, may hold values from -60 to 60
- new_kv: bfloat16 [32, 2048], P(('groups', 'kvb')), parts along dimension 0, may hold values from -6 to 6
- kv_cache: bfloat16 [2048, 16, 2048], P(('groups', 'kvb', 'tp')), parts along dimension 0, may hold values from -6 to 6
- lengths: int32 [32], P('groups'), parts along dimension 0, may hold values from 1 to 2048, as said below
- slot_seq: int32 [2048], P(('groups', 'kvb', 'tp')), parts along dimension 0, may hold values from 0 to 15, as said below
- slot_block: int32 [2048], P(('groups', 'kvb', 'tp')), parts along dimension 0, may hold values from 0 to 127, as said below
- block_counts: int32 [32], P(('groups', 'kvb', 'tp')), parts along dimension 0, may hold values from 16 to 64, as said below
- out_weight: bfloat16 [8192, 8192], P('tp'), may hold values from -0.5 to 0.5
- norm_gain: bfloat16 [8192], P('tp'), may hold values from 0.099609375 to 1.8984375
Outputs:
- stream: bfloat16 [32, 8192], P(('groups', 'kvb'), 'tp'), parts along dimension 0
- normed: bfloat16 [32, 8192], P(('groups', 'kvb'), 'tp'), parts along dimension 0
There are 2 independent parts, one for each index of `groups`. A program takes and returns all parts, laid end to end along the dimension named above; an argument that names none is the same for every part. Nothing has to cross between parts.
Inputs may be any that keep to these rules, and one draw needn't show every extreme that they name: `block_counts`: slots below a device's count hold cache blocks, those at or beyond it none; at least one device's count is 64. `slot_seq`: each pair of a sequence s and a block b below ceil(lengths[s] / 16) sits in exactly one live slot of the group. `slot_block`: some sequence has exactly 128 blocks; none has more. `lengths`: some sequence has exactly 16 * (128) tokens.
All inputs are finite; a program needn't handle non-finite values.
Results may differ from a plain program's by a relative error of at most 0.006.
Values may be sent and summed in bfloat16 or wider, within the bound.
No kernel may reach another device: no remote copies, remote signals or barrier semaphores. Data moves between devices by JAX's collectives and lax.ppermute only.
A program may use at most 64 MiB of HBM per device.

v0:
```python
import jax
import jax.numpy as jnp
from jax import lax
from jax.sharding import PartitionSpec as P

QH = 64
KVH = 8
HD = 128
BLK = 16
NEGATIVE = -1e30
EPSILON = 1e-06


def on_device(
    residual,
    queries,
    new_kv,
    kv_cache,
    lengths,
    slot_seq,
    slot_block,
    block_counts,
    out_weight,
    norm_gain,
):
    tp_count = lax.axis_size("tp")
    kvb_count = lax.axis_size("kvb")
    tp_index = lax.axis_index("tp")
    seq_rep = residual.shape[0]
    local_heads = queries.shape[1] // HD
    group_size = QH // KVH
    score_scale = HD ** (-0.5)
    wide = lax.all_gather(queries, "tp", axis=1, tiled=True)
    every = lax.all_gather(wide, "kvb", axis=0, tiled=True)
    seq_total = every.shape[0]
    grouped = every.reshape(seq_total, KVH, group_size, HD)
    pool_size = kv_cache.shape[0]
    step_slots = min(32, pool_size)
    live_count = block_counts[0]
    seq_ids = jnp.arange(seq_total, dtype=jnp.int32)
    offsets = jnp.arange(BLK, dtype=jnp.int32)

    def advance(turn_index, carried):
        peak_now, weight_sum, partial_rows = carried
        first_slot = turn_index * step_slots
        cache_part = lax.dynamic_slice_in_dim(kv_cache, first_slot, step_slots, 0)
        seq_part = lax.dynamic_slice_in_dim(slot_seq, first_slot, step_slots, 0)
        block_part = lax.dynamic_slice_in_dim(slot_block, first_slot, step_slots, 0)
        key_rows = cache_part[:, :, : KVH * HD].reshape(step_slots * BLK, KVH, HD)
        value_rows = cache_part[:, :, KVH * HD :].reshape(step_slots * BLK, KVH, HD)
        token_seq = jnp.repeat(seq_part, BLK)
        position = (block_part[:, None] * BLK + offsets[None, :]).reshape(-1)
        slot_live = jnp.repeat(
            first_slot + jnp.arange(step_slots, dtype=jnp.int32) < live_count, BLK
        )
        member = token_seq[None, :] == seq_ids[:, None]
        length_of = jnp.sum(jnp.where(member, lengths[:, None], 0), axis=0)
        live = member & (position < length_of)[None, :] & slot_live[None, :]
        mask = live[:, None, None, :]
        scores = (
            jnp.einsum("sgqd,ngd->sgqn", grouped, key_rows, preferred_element_type=jnp.float32)
            * score_scale
        )
        peak_next = jnp.maximum(peak_now, jnp.max(jnp.where(mask, scores, NEGATIVE), axis=-1))
        weights = jnp.where(mask, jnp.exp(scores - peak_next[..., None]), 0.0)
        shrink = jnp.exp(peak_now - peak_next)
        weight_sum = weight_sum * shrink + jnp.sum(weights, axis=-1)
        partial_rows = partial_rows * shrink[..., None] + jnp.einsum(
            "sgqn,ngd->sgqd",
            weights.astype(jnp.bfloat16),
            value_rows,
            preferred_element_type=jnp.float32,
        )
        return (peak_next, weight_sum, partial_rows)

    start_state = (
        jnp.full((seq_total, KVH, group_size), NEGATIVE, jnp.float32),
        jnp.zeros((seq_total, KVH, group_size), jnp.float32),
        jnp.zeros((seq_total, KVH, group_size, HD), jnp.float32),
    )
    turn_count = (live_count + step_slots - 1) // step_slots
    peak_now, weight_sum, partial_rows = lax.fori_loop(0, turn_count, advance, start_state)
    row_out = partial_rows.reshape(kvb_count, seq_rep, tp_count, local_heads * HD).transpose(
        0, 2, 1, 3
    )
    peak_out = peak_now.reshape(kvb_count, seq_rep, tp_count, local_heads).transpose(0, 2, 1, 3)
    sum_out = weight_sum.reshape(kvb_count, seq_rep, tp_count, local_heads).transpose(0, 2, 1, 3)
    device_total = kvb_count * tp_count
    got_rows, got_peaks, got_sums = (
        lax.all_to_all(
            row_out.reshape(device_total, seq_rep, local_heads * HD),
            ("kvb", "tp"),
            split_axis=0,
            concat_axis=0,
            tiled=True,
        ),
        lax.all_to_all(
            peak_out.reshape(device_total, seq_rep, local_heads),
            ("kvb", "tp"),
            split_axis=0,
            concat_axis=0,
            tiled=True,
        ),
        lax.all_to_all(
            sum_out.reshape(device_total, seq_rep, local_heads),
            ("kvb", "tp"),
            split_axis=0,
            concat_axis=0,
            tiled=True,
        ),
    )
    got_rows = got_rows.reshape(device_total, seq_rep, local_heads, HD)
    kv_local = max(1, local_heads // group_size)
    per_kv = local_heads // kv_local
    kv_first = tp_index * local_heads // group_size
    new_keys = lax.dynamic_slice_in_dim(new_kv, kv_first * HD, kv_local * HD, 1).reshape(
        seq_rep, kv_local, HD
    )
    new_values = lax.dynamic_slice_in_dim(new_kv, KVH * HD + kv_first * HD, kv_local * HD, 1)
    new_values = new_values.reshape(seq_rep, kv_local, 1, HD).astype(jnp.float32)
    own_view = queries.reshape(seq_rep, kv_local, per_kv, HD)
    fresh = (
        jnp.einsum("rkqd,rkd->rkq", own_view, new_keys, preferred_element_type=jnp.float32)
        * score_scale
    )
    fresh = fresh.reshape(seq_rep, local_heads)
    fresh_values = jnp.broadcast_to(new_values, (seq_rep, kv_local, per_kv, HD)).reshape(
        seq_rep, local_heads, HD
    )
    overall = jnp.maximum(jnp.max(got_peaks, axis=0), fresh)
    scaling = jnp.exp(got_peaks - overall[None])
    fresh_weight = jnp.exp(fresh - overall)
    denominator = jnp.sum(scaling * got_sums, axis=0) + fresh_weight
    numerator = (
        jnp.sum(scaling[..., None] * got_rows, axis=0) + fresh_weight[..., None] * fresh_values
    )
    attended = (
        (numerator / denominator[..., None]).reshape(seq_rep, local_heads * HD).astype(jnp.bfloat16)
    )
    projected = jnp.dot(attended, out_weight, preferred_element_type=jnp.float32)
    width_dev = norm_gain.shape[0]
    column = tp_index * width_dev
    summed = lax.psum(projected, "tp")
    full_stream = (residual.astype(jnp.float32) + summed).astype(jnp.bfloat16)
    full_wide = lax.optimization_barrier(full_stream).astype(jnp.float32)
    mean_square = jnp.mean(full_wide * full_wide, axis=1)
    stream = lax.dynamic_slice_in_dim(full_stream, column, width_dev, 1)
    stream_wide = lax.dynamic_slice_in_dim(full_wide, column, width_dev, 1)
    normed = (
        stream_wide * lax.rsqrt(mean_square + EPSILON)[:, None] * norm_gain.astype(jnp.float32)
    ).astype(jnp.bfloat16)
    return (stream, normed)


def solution(mesh):
    placed = (
        P(("groups", "kvb"), None),
        P(("groups", "kvb"), "tp"),
        P(("groups", "kvb"), None),
        P(("groups", "kvb", "tp"), None, None),
        P("groups"),
        P(("groups", "kvb", "tp")),
        P(("groups", "kvb", "tp")),
        P(("groups", "kvb", "tp")),
        P("tp", None),
        P("tp"),
    )
    return jax.shard_map(
        on_device,
        mesh=mesh,
        in_specs=placed,
        out_specs=(P(("groups", "kvb"), "tp"), P(("groups", "kvb"), "tp")),
        check_vma=False,
    )
```

profile of v0, /device:TPU:0, one launch (start us, length us, event | category | flops | bytes accessed | tf_op | source)
XLA Modules:
  0.0 138.4 jit_solution(4578274907591061050)
XLA Ops:
  7.8 6.5 %all_gather.6 = bf16[4,8192]{1,0:T(4,128)(2,1)S(1)} all-gather(bf16[4,2048]{1,0:T(4,128)(2,1)} %param.13), channel_id=1, replica_groups=mesh['groups'=2,'kvb'=4,'tp'=4] {'tp'}, dimensions={1}, use_global_device_ids=true | all-gather | bytes 81920 | tf_op jit(solution)/shard_map/all_gather | solution.py:33
  14.3 14.5 %all-gather = bf16[4,4,8192]{2,1,0:T(4,128)(2,1)S(1)} all-gather(bf16[1,4,8192]{2,1,0:T(4,128)(2,1)S(1)} %bitcast.100), channel_id=1, replica_groups=mesh['groups'=2,'kvb'=4,'tp'=4] {'kvb'}, dimensions={0}, use_global_device_ids=true | all-gather | bytes 327680 | tf_op jit(solution)/shard_map/all_gather | solution.py:34
  29.4 7.9 %while.17 = (s32[]{:T(128)}, f32[16,8,8]{0,2,1:T(8,128)S(1)}, f32[16,8,8]{0,2,1:T(8,128)S(1)}, f32[16,8,8,128]{3,0,2,1:T(8,128)S(1)}, s32[]{:T(128)}, /*index=5*...) while((s32[]{:T(128)}, f32[16,8,8]{0,2,1:T(8,128)S(1)}, ...), condition=%wide.region_4.5_spmd.clone.clone, body=%wide.region_0.4_spmd.clone.clone.sunk | while | flops 274516576 | bytes 18212968 | solution.py:82
  29.4 0.7 dynamic_slice.42
  30.3 0.7 fusion.44
  31.1 0.7 dynamic-slice_multiply_fusion.2
  32.0 0.7 add_compare_fusion.2
  32.8 1.7 %constant_dynamic-slice_fusion.5 = (bf16[32,16,1024]{2,1,0:T(8,128)(2,1)S(1)}, bf16[32,16,1024]{2,1,0:T(8,128)(2,1)S(1)}) fusion(bf16[64,16,2048]{2,1,0:T(8,128)(2,1)} %get-tuple-element.348, s32[]{:T(128)S(6)} %select_n.72, s32[]{:T(128)S(6)} %add.157), kind=kLoop, calls=%fused_computation.28.clone.1 | loop fusion | bytes 4194312 | tf_op jit(solution)/shard_map/while/body/slice | solution.py:50
  35.4 0.6 fusion.47
  36.3 0.9 fusion.48
  38.1 12.3 %all-to-all-start = ((f32[16,4,16]{2,1,0:T(4,128)}), f32[16,4,16]{2,1,0:T(4,128)S(1)}, u32[]{:S(2)}, u32[]{:S(2)}) async-start(f32[16,4,16]{2,1,0:T(4,128)} %copy.36), calls=%async_computation | async-start | bytes 65536 | tf_op jit(solution)/shard_map/all_to_all | solution.py:97
  50.4 0.7 dynamic-slice_convert_fusion
  51.3 0.6 copy.41
  52.0 5.1 %all-to-all-done = f32[16,4,16]{2,1,0:T(4,128)S(1)} async-done(((f32[16,4,16]{2,1,0:T(4,128)}), f32[16,4,16]{2,1,0:T(4,128)S(1)}, u32[]{:S(2)}, u32[]{:S(2)}) %all-to-all-start) | async-done | bytes 4128 | tf_op jit(solution)/shard_map/all_to_all | solution.py:97
  57.0 3.5 %all-to-all-start.2 = ((f32[16,4,16]{2,1,0:T(4,128)}), f32[16,4,16]{2,1,0:T(4,128)S(1)}, u32[]{:S(2)}, u32[]{:S(2)}) async-start(f32[16,4,16]{2,1,0:T(4,128)} %copy.41), calls=%async_computation.2 | async-start | bytes 65536 | tf_op jit(solution)/shard_map/all_to_all | solution.py:104
  61.0 1.1 copy.38
  62.2 5.0 %all-to-all-done.2 = f32[16,4,16]{2,1,0:T(4,128)S(1)} async-done(((f32[16,4,16]{2,1,0:T(4,128)}), f32[16,4,16]{2,1,0:T(4,128)S(1)}, u32[]{:S(2)}, u32[]{:S(2)}) %all-to-all-start.2) | async-done | bytes 4128 | tf_op jit(solution)/shard_map/all_to_all | solution.py:104
  67.1 3.6 %all-to-all-start.1 = ((f32[16,4,2048]{2,1,0:T(4,128)}), f32[16,4,2048]{2,1,0:T(4,128)S(1)}, u32[]{:S(2)}, u32[]{:S(2)}) async-start(f32[16,4,2048]{2,1,0:T(4,128)} %bitcast.7), calls=%async_computation.1 | async-start | bytes 1048576 | tf_op jit(solution)/shard_map/all_to_all | solution.py:90
  71.4 13.5 %all-to-all-done.1 = f32[16,4,2048]{2,1,0:T(4,128)S(1)} async-done(((f32[16,4,2048]{2,1,0:T(4,128)}), f32[16,4,2048]{2,1,0:T(4,128)S(1)}, u32[]{:S(2)}, u32[]{:S(2)}) %all-to-all-start.1) | async-done | bytes 524320 | tf_op jit(solution)/shard_map/all_to_all | solution.py:90
  85.1 13.5 %fusion.24 = f32[4,8192]{1,0:T(4,128)} fusion(bf16[2048,8192]{1,0:T(8,128)(2,1)} %param.20, f32[1,4,16,128]{3,2,1,0:T(8,128)S(1)} %get-tuple-element.225, f32[4,2048]{1,0:T(4,128)S(1)} %multiply_reduce_fusion, f32[1,4,16,128]{3,2,1,0:T(8,128)S(1)} %broadcast_bitcast_fusion.1, f32[1,4,16,128]{3,2,1,0:T(8,128)S(1)} %get-tuple-element.226), kind=kOutput, calls=%fused_computation.41 | convolution fusion | flops 134250496 | bytes 33816576 | tf_op jit(solution)/shard_map/dot_general | solution.py:140
  98.7 30.4 %all-reduce.2.cloned.1.call-done = f32[4,8192]{1,0:T(4,128)} async-done(((f32[4,8192]{1,0:T(4,128)}), f32[4,8192]{1,0:T(4,128)}) %all-reduce.2.cloned.1.call-update) | async-done | bytes 131088 | tf_op jit(solution)/shard_map/psum | solution.py:143
  129.1 0.9 add_convert_fusion
  130.3 0.6 constant_dynamic-slice_fusion.2
  130.9 0.7 multiply_convert_fusion
  (54 shorter events, 4.7 us)
Async XLA Ops:
  29.4 31.2 %copy-start.1 = (bf16[4,2048]{1,0:T(4,128)(2,1)S(1)}, bf16[4,2048]{1,0:T(4,128)(2,1)}, u32[]{:S(2)}) copy-start(bf16[4,2048]{1,0:T(4,128)(2,1)} %param.13) | copy-start | bytes 49156
  38.1 18.9 %all-to-all-start = ((f32[16,4,16]{2,1,0:T(4,128)}), f32[16,4,16]{2,1,0:T(4,128)S(1)}, u32[]{:S(2)}, u32[]{:S(2)}) async-start(f32[16,4,16]{2,1,0:T(4,128)} %copy.36), calls=%async_computation | async-start | bytes 65536 | tf_op jit(solution)/shard_map/all_to_all | solution.py:97
  57.0 10.1 %all-to-all-start.2 = ((f32[16,4,16]{2,1,0:T(4,128)}), f32[16,4,16]{2,1,0:T(4,128)S(1)}, u32[]{:S(2)}, u32[]{:S(2)}) async-start(f32[16,4,16]{2,1,0:T(4,128)} %copy.41), calls=%async_computation.2 | async-start | bytes 65536 | tf_op jit(solution)/shard_map/all_to_all | solution.py:104
  67.1 17.8 %all-to-all-start.1 = ((f32[16,4,2048]{2,1,0:T(4,128)}), f32[16,4,2048]{2,1,0:T(4,128)S(1)}, u32[]{:S(2)}, u32[]{:S(2)}) async-start(f32[16,4,2048]{2,1,0:T(4,128)} %bitcast.7), calls=%async_computation.1 | async-start | bytes 1048576 | tf_op jit(solution)/shard_map/all_to_all | solution.py:90
  70.7 58.4 %all-reduce.2.cloned.1.call-start = ((), (), s32[]{:S(2)}) async-start(), calls=%async_computation.3 | async-start | bytes 262144 | tf_op jit(solution)/shard_map/psum | solution.py:143
  85.1 13.6 %copy-start.2 = (bf16[2048]{0:T(1024)(128)(2,1)S(1)}, bf16[2048]{0:T(1024)(128)(2,1)}, u32[]{:S(2)}) copy-start(bf16[2048]{0:T(1024)(128)(2,1)} %param.21) | copy-start | bytes 12292
  85.1 44.0 %copy-start = (bf16[4,8192]{1,0:T(4,128)(2,1)S(1)}, bf16[4,8192]{1,0:T(4,128)(2,1)}, u32[]{:S(2)}) copy-start(bf16[4,8192]{1,0:T(4,128)(2,1)} %param.12) | copy-start | bytes 196612
Sparse Core Ops, SparseCore 0:
  98.8 30.2 all-reduce.1
where the time goes:
time: 139 us; the launch traced here: 138 us
  waiting for transfers between devices  54 us (39%)
  blocking collectives  21 us (15%)
  starting transfers between devices  19.4 us (14%)
  matrix products  15.1 us (11%)
  between operations  14.9 us (11%)
  local copies, waits for them, and re-layouts  8.16 us (6%)
  other arithmetic  5.66 us (4%)
    psum x1, waiting for transfers between devices, on_device(): summed = lax.psum(projected, 'tp')  30.4 us
    all_gather x1, blocking collectives, on_device(): every = lax.all_gather(wide, 'kvb', axis=0, tiled=True)  14.5 us
    dot_general x1, matrix products, on_device(): jnp.dot(attended, out_weight, preferred_element_type=jnp.float32)  13.5 us
    all_to_all x1, waiting for transfers between devices, on_device(): lax.all_to_all(row_out.reshape(device_total, seq_rep, local_heads * HD),...  13.5 us
    all_to_all x1, starting transfers between devices, on_device(): lax.all_to_all(peak_out.reshape(device_total, seq_rep, local_heads), ('kv...  12.3 us
    all_gather x1, blocking collectives, on_device(): wide = lax.all_gather(queries, 'tp', axis=1, tiled=True)  6.46 us
    all_to_all x1, waiting for transfers between devices, on_device(): lax.all_to_all(peak_out.reshape(device_total, seq_rep, local_heads), ('kv...  5.08 us
    all_to_all x1, waiting for transfers between devices, on_device(): lax.all_to_all(sum_out.reshape(device_total, seq_rep, local_heads), ('kvb...  4.97 us
  transfers between devices with their start and end apart: 4, of which 4 were waited for; matrix products, arithmetic and copies ran while one was open for 3% of the time, Pallas kernels for 0%

commit v1 on v0

--- a/solution.py
+++ b/solution.py
@@ -140,7 +140,7 @@
     projected = jnp.dot(attended, out_weight, preferred_element_type=jnp.float32)
     width_dev = norm_gain.shape[0]
     column = tp_index * width_dev
-    summed = lax.psum(projected, "tp")
+    summed = jnp.sum(lax.all_gather(projected, "tp"), axis=0)
     full_stream = (residual.astype(jnp.float32) + summed).astype(jnp.bfloat16)
     full_wide = lax.optimization_barrier(full_stream).astype(jnp.float32)
     mean_square = jnp.mean(full_wide * full_wide, axis=1)

time: 139 us -> 101 us (0.73)
  waiting for transfers between devices: 54 us -> 23.6 us
  between operations: 14.9 us -> 1.55 us
  blocking collectives: 21 us -> 28 us
    psum x1 -> x0, waiting for transfers between devices: 30.4 us -> none  [on_device(): summed = lax.psum(projected, 'tp')]
    all_gather x0 -> x1, blocking collectives: none -> 7.04 us  [on_device(): summed = jnp.sum(lax.all_gather(projected, 'tp'), axis=0)]
  transfers between devices with their start and end apart: 4 -> 3, of which waited for: 4 -> 3; matrix products, arithmetic and copies ran while one was open for 3% -> 4% of each run, Pallas kernels for 0% -> 0%
where the time goes in v1:
time: 101 us; the launch traced here: 100 us
  blocking collectives  28 us (28%)
  waiting for transfers between devices  23.6 us (23%)
  starting transfers between devices  19.4 us (19%)
  matrix products  14.5 us (14%)
  local copies, waits for them, and re-layouts  8.15 us (8%)
  other arithmetic  4.86 us (5%)
  between operations  1.55 us (2%)
    all_gather x1, blocking collectives, on_device(): every = lax.all_gather(wide, 'kvb', axis=0, tiled=True)  14.5 us
    all_to_all x1, waiting for transfers between devices, on_device(): lax.all_to_all(row_out.reshape(device_total, seq_rep, local_heads * HD),...  13.6 us
    dot_general x1, matrix products, on_device(): jnp.dot(attended, out_weight, preferred_element_type=jnp.float32)  12.9 us
    all_to_all x1, starting transfers between devices, on_device(): lax.all_to_all(peak_out.reshape(device_total, seq_rep, local_heads), ('kv...  12.3 us
    all_gather x1, blocking collectives, on_device(): summed = jnp.sum(lax.all_gather(projected, 'tp'), axis=0)  7.04 us
    all_gather x1, blocking collectives, on_device(): wide = lax.all_gather(queries, 'tp', axis=1, tiled=True)  6.46 us
    all_to_all x1, waiting for transfers between devices, on_device(): lax.all_to_all(peak_out.reshape(device_total, seq_rep, local_heads), ('kv...  5.08 us
    all_to_all x1, waiting for transfers between devices, on_device(): lax.all_to_all(sum_out.reshape(device_total, seq_rep, local_heads), ('kvb...  4.97 us
  transfers between devices with their start and end apart: 3, of which 3 were waited for; matrix products, arithmetic and copies ran while one was open for 4% of the time, Pallas kernels for 0%

profile of v1, /device:TPU:0, one launch (start us, length us, event | category | flops | bytes accessed | tf_op | source)
XLA Modules:
  0.0 100.2 jit_solution(5673422876722209004)
XLA Ops:
  1.3 6.5 %all_gather.12 = bf16[4,8192]{1,0:T(4,128)(2,1)S(1)} all-gather(bf16[4,2048]{1,0:T(4,128)(2,1)} %param.13), channel_id=1, replica_groups=mesh['groups'=2,'kvb'=4,'tp'=4] {'tp'}, dimensions={1}, use_global_device_ids=true | all-gather | bytes 81920 | tf_op jit(solution)/shard_map/all_gather | solution.py:33
  7.7 14.5 %all-gather.1 = bf16[4,4,8192]{2,1,0:T(4,128)(2,1)S(1)} all-gather(bf16[1,4,8192]{2,1,0:T(4,128)(2,1)S(1)} %bitcast.102), channel_id=1, replica_groups=mesh['groups'=2,'kvb'=4,'tp'=4] {'kvb'}, dimensions={0}, use_global_device_ids=true | all-gather | bytes 327680 | tf_op jit(solution)/shard_map/all_gather | solution.py:34
  22.9 7.9 %while.17 = (s32[]{:T(128)}, f32[16,8,8]{0,2,1:T(8,128)S(1)}, f32[16,8,8]{0,2,1:T(8,128)S(1)}, f32[16,8,8,128]{3,0,2,1:T(8,128)S(1)}, s32[]{:T(128)}, /*index=5*...) while((s32[]{:T(128)}, f32[16,8,8]{0,2,1:T(8,128)S(1)}, ...), condition=%wide.region_4.5_spmd.clone.clone, body=%wide.region_0.4_spmd.clone.clone.sunk | while | flops 274516576 | bytes 18212968 | solution.py:82
  22.9 0.7 dynamic_slice.42
  23.8 0.7 fusion.43
  24.5 0.7 dynamic-slice_multiply_fusion.2
  25.4 0.7 add_compare_fusion.2
  26.3 1.7 %constant_dynamic-slice_fusion.5 = (bf16[32,16,1024]{2,1,0:T(8,128)(2,1)S(1)}, bf16[32,16,1024]{2,1,0:T(8,128)(2,1)S(1)}) fusion(bf16[64,16,2048]{2,1,0:T(8,128)(2,1)} %get-tuple-element.348, s32[]{:T(128)S(6)} %select_n.72, s32[]{:T(128)S(6)} %add.155), kind=kLoop, calls=%fused_computation.28.clone.1 | loop fusion | bytes 4194312 | tf_op jit(solution)/shard_map/while/body/slice | solution.py:50
  28.9 0.6 fusion.46
  29.8 0.9 fusion.47
  30.9 0.6 copy.36
  31.6 12.3 %all-to-all-start = ((f32[16,4,16]{2,1,0:T(4,128)}), f32[16,4,16]{2,1,0:T(4,128)S(1)}, u32[]{:S(2)}, u32[]{:S(2)}) async-start(f32[16,4,16]{2,1,0:T(4,128)} %copy.36), calls=%async_computation | async-start | bytes 65536 | tf_op jit(solution)/shard_map/all_to_all | solution.py:97
  43.9 0.7 dynamic-slice_convert_fusion
  44.8 0.6 copy.41
  45.4 5.1 %all-to-all-done = f32[16,4,16]{2,1,0:T(4,128)S(1)} async-done(((f32[16,4,16]{2,1,0:T(4,128)}), f32[16,4,16]{2,1,0:T(4,128)S(1)}, u32[]{:S(2)}, u32[]{:S(2)}) %all-to-all-start) | async-done | bytes 4128 | tf_op jit(solution)/shard_map/all_to_all | solution.py:97
  50.5 3.5 %all-to-all-start.2 = ((f32[16,4,16]{2,1,0:T(4,128)}), f32[16,4,16]{2,1,0:T(4,128)S(1)}, u32[]{:S(2)}, u32[]{:S(2)}) async-start(f32[16,4,16]{2,1,0:T(4,128)} %copy.41), calls=%async_computation.2 | async-start | bytes 65536 | tf_op jit(solution)/shard_map/all_to_all | solution.py:104
  54.5 1.1 %copy.38 = f32[4,4,4,2048]{3,2,1,0:T(4,128)} copy(f32[4,4,4,2048]{3,1,2,0:T(4,128)S(1)} %bitcast.101) | data formatting | bytes 1048576 | tf_op jit(solution)/shard_map/transpose | solution.py:83
  55.6 5.0 %all-to-all-done.2 = f32[16,4,16]{2,1,0:T(4,128)S(1)} async-done(((f32[16,4,16]{2,1,0:T(4,128)}), f32[16,4,16]{2,1,0:T(4,128)S(1)}, u32[]{:S(2)}, u32[]{:S(2)}) %all-to-all-start.2) | async-done | bytes 4128 | tf_op jit(solution)/shard_map/all_to_all | solution.py:104
  60.6 3.6 %all-to-all-start.1 = ((f32[16,4,2048]{2,1,0:T(4,128)}), f32[16,4,2048]{2,1,0:T(4,128)S(1)}, u32[]{:S(2)}, u32[]{:S(2)}) async-start(f32[16,4,2048]{2,1,0:T(4,128)} %bitcast.7), calls=%async_computation.1 | async-start | bytes 1048576 | tf_op jit(solution)/shard_map/all_to_all | solution.py:90
  64.9 13.6 %all-to-all-done.1 = f32[16,4,2048]{2,1,0:T(4,128)S(1)} async-done(((f32[16,4,2048]{2,1,0:T(4,128)}), f32[16,4,2048]{2,1,0:T(4,128)S(1)}, u32[]{:S(2)}, u32[]{:S(2)}) %all-to-all-start.1) | async-done | bytes 524320 | tf_op jit(solution)/shard_map/all_to_all | solution.py:90
  78.6 12.9 %convolution_bitcast_fusion.1 = f32[1,4,8192]{2,1,0:T(4,128)S(1)} fusion(bf16[2048,8192]{1,0:T(8,128)(2,1)} %param.20, f32[1,4,16,128]{3,2,1,0:T(8,128)S(1)} %get-tuple-element.225, f32[4,2048]{1,0:T(4,128)S(1)} %multiply_reduce_fusion, f32[1,4,16,128]{3,2,1,0:T(8,128)S(1)} %broadcast_bitcast_fusion.1, f32[1,4,16,128]{3,2,1,0:T(8,128)S(1)} %get-tuple-element.226), kind=kOutput, calls=%fused_computation.31 | convolution fusion | flops 134250496 | bytes 33816576 | tf_op jit(solution)/shard_map/dot_general | solution.py:140
  91.5 7.0 %all-gather.2 = f32[4,4,8192]{2,1,0:T(4,128)S(1)} all-gather(f32[1,4,8192]{2,1,0:T(4,128)S(1)} %convolution_bitcast_fusion.1), channel_id=2, replica_groups=mesh['groups'=2,'kvb'=4,'tp'=4] {'tp'}, dimensions={0}, use_global_device_ids=true | all-gather | bytes 655360 | tf_op jit(solution)/shard_map/all_gather | solution.py:143
  98.9 0.6 constant_dynamic-slice_fusion.2
  99.5 0.7 multiply_convert_fusion
  (53 shorter events, 4.1 us)
Async XLA Ops:
  22.9 31.2 %copy-start.1 = (bf16[4,2048]{1,0:T(4,128)(2,1)S(1)}, bf16[4,2048]{1,0:T(4,128)(2,1)}, u32[]{:S(2)}) copy-start(bf16[4,2048]{1,0:T(4,128)(2,1)} %param.13) | copy-start | bytes 49156
  31.6 18.9 %all-to-all-start = ((f32[16,4,16]{2,1,0:T(4,128)}), f32[16,4,16]{2,1,0:T(4,128)S(1)}, u32[]{:S(2)}, u32[]{:S(2)}) async-start(f32[16,4,16]{2,1,0:T(4,128)} %copy.36), calls=%async_computation | async-start | bytes 65536 | tf_op jit(solution)/shard_map/all_to_all | solution.py:97
  50.5 10.1 %all-to-all-start.2 = ((f32[16,4,16]{2,1,0:T(4,128)}), f32[16,4,16]{2,1,0:T(4,128)S(1)}, u32[]{:S(2)}, u32[]{:S(2)}) async-start(f32[16,4,16]{2,1,0:T(4,128)} %copy.41), calls=%async_computation.2 | async-start | bytes 65536 | tf_op jit(solution)/shard_map/all_to_all | solution.py:104
  54.1 10.2 %copy-start.2 = (bf16[2048]{0:T(1024)(128)(2,1)S(1)}, bf16[2048]{0:T(1024)(128)(2,1)}, u32[]{:S(2)}) copy-start(bf16[2048]{0:T(1024)(128)(2,1)} %param.21) | copy-start | bytes 12292
  60.6 17.8 %all-to-all-start.1 = ((f32[16,4,2048]{2,1,0:T(4,128)}), f32[16,4,2048]{2,1,0:T(4,128)S(1)}, u32[]{:S(2)}, u32[]{:S(2)}) async-start(f32[16,4,2048]{2,1,0:T(4,128)} %bitcast.7), calls=%async_computation.1 | async-start | bytes 1048576 | tf_op jit(solution)/shard_map/all_to_all | solution.py:90
  78.6 20.0 %copy-start = (bf16[4,8192]{1,0:T(4,128)(2,1)S(1)}, bf16[4,8192]{1,0:T(4,128)(2,1)}, u32[]{:S(2)}) copy-start(bf16[4,8192]{1,0:T(4,128)(2,1)} %param.12) | copy-start | bytes 196612
